TPU v7x, 32 devices: a whole 2x2x4 slice. The times are simulated.
32 devices in a mesh: seq: 16 (over z, y, x), rep: 2 (over core).
Axes of the slice: x: 2, y: 2, z: 4, core: 2. Of those that a mesh axis runs over, the one named last changes fastest.
Arguments:
- q_lin: bfloat16 [2, 2048, 4096], P('rep', 'seq'), may hold values from -90 to 90, as said below
- k_lin: bfloat16 [2, 2048, 512], P('rep', 'seq'), may hold values from -4 to 4
- value_projection: bfloat16 [2, 2048, 512], P('rep', 'seq'), may hold values from -6 to 6
- grad_out: bfloat16 [2, 2048, 4096], P('rep', 'seq'), may hold values from -6 to 6
- q_bias: float32 [4096], replicated, may hold values from -3 to 3
- block_lists: int32 [32, 16, 2], replicated, may hold values from 0 to 15, as said below
- block_counts: int32 [32, 16], replicated, may hold values from 1 to 2, as said below
Outputs:
- dq: bfloat16 [2, 2048, 4096], P('rep', 'seq')
- dk: bfloat16 [2, 2048, 512], P('rep', 'seq')
- dv: bfloat16 [2, 2048, 512], P('rep', 'seq')
- dbq: float32 [4096], replicated
Inputs may be any that keep to these rules, and one draw needn't show every extreme that they name: `q_lin`: in the shown and hidden draws alike the entries stay within the stated range. `block_lists`: entry 0 of every list is the query block itself; the 2 entries of a list are distinct; entries past block_counts are ignored. `block_counts`: some head has 2 for every query block.
All inputs are finite; a program needn't handle non-finite values.
Results may differ from a plain program's by a relative error of at most 0.008.
Values may be sent and summed in bfloat16 or wider, within the bound.
A program may use at most 128 MiB of HBM per device.

v0:
```python
import jax
import jax.numpy as jnp
from jax import lax
from jax.sharding import PartitionSpec as P

masked_score = -1e30


def unit_layout(values_in, part_count, slice_rows, head_count, head_dim):
    shaped = values_in.reshape(part_count, slice_rows, head_count, head_dim)
    return jnp.transpose(shaped, (1, 2, 0, 3)).reshape(
        slice_rows, head_count * part_count, head_dim
    )


def tile_pass(query_rows, grads, chosen, counts, key_blocks, value_blocks, scaling):
    tile_count, row_count, head_dim = query_rows.shape
    list_width = chosen.shape[1]
    block_total, block_rows, _ = key_blocks.shape
    key_tiles = jnp.take(key_blocks, chosen, axis=0).reshape(
        tile_count, list_width * block_rows, head_dim
    )
    value_tiles = jnp.take(value_blocks, chosen, axis=0).reshape(
        tile_count, list_width * block_rows, head_dim
    )
    active = jnp.repeat(
        jnp.arange(list_width, dtype=jnp.int32)[None, :] < counts[:, None], block_rows, axis=1
    )
    scores = (
        jnp.einsum("tqd,tkd->tqk", query_rows, key_tiles, preferred_element_type=jnp.float32)
        * scaling
    )
    scores = jnp.where(active[:, None, :], scores, masked_score)
    weights = jax.nn.softmax(scores, axis=-1)
    weights_half = weights.astype(jnp.bfloat16)
    attn_out = jnp.einsum(
        "tqk,tkd->tqd", weights_half, value_tiles, preferred_element_type=jnp.float32
    )
    row_dots = jnp.sum(grads.astype(jnp.float32) * attn_out, axis=2)
    weight_grads = jnp.einsum(
        "tqd,tkd->tqk", grads, value_tiles, preferred_element_type=jnp.float32
    )
    score_grads = (weights * (weight_grads - row_dots[:, :, None])).astype(jnp.bfloat16)
    grad_q = scaling * jnp.einsum(
        "tqk,tkd->tqd", score_grads, key_tiles, preferred_element_type=jnp.float32
    )
    key_update = scaling * jnp.einsum(
        "tqk,tqd->tkd", score_grads, query_rows, preferred_element_type=jnp.float32
    )
    value_update = jnp.einsum(
        "tqk,tqd->tkd", weights_half, grads, preferred_element_type=jnp.float32
    )
    selector = (
        chosen.reshape(tile_count * list_width)[:, None]
        == jnp.arange(block_total, dtype=jnp.int32)[None, :]
    ).astype(jnp.float32)
    key_gradient = jnp.einsum(
        "mn,mrd->nrd",
        selector,
        key_update.reshape(tile_count * list_width, block_rows, head_dim),
        precision=lax.Precision.HIGHEST,
        preferred_element_type=jnp.float32,
    )
    value_gradient = jnp.einsum(
        "mn,mrd->nrd",
        selector,
        value_update.reshape(tile_count * list_width, block_rows, head_dim),
        precision=lax.Precision.HIGHEST,
        preferred_element_type=jnp.float32,
    )
    return (grad_q, key_gradient, value_gradient)


def body(q_lin, k_lin, value_projection, grad_out, q_bias, block_lists, block_counts):
    devices = lax.axis_size("seq")
    my_index = lax.axis_index("seq")
    tok_rows = q_lin.shape[1]
    head_count, qblock_count, list_width = block_lists.shape
    head_dim = q_bias.shape[0] // head_count
    kv_count = k_lin.shape[2] // head_dim
    part_count = 2 * devices // head_count
    slice_rows = tok_rows // part_count
    block_rows = tok_rows * devices // qblock_count
    tile_rows = min(slice_rows, block_rows)
    per_slice = slice_rows // tile_rows
    tile_count = devices * per_slice
    unit_count = head_count * part_count
    scaling = head_dim ** (-0.5)
    placing = jnp.arange(unit_count, dtype=jnp.int32)
    joined = part_count % 2 == 0 and block_rows % (2 * slice_rows) == 0
    query_rows = (q_lin[0].astype(jnp.float32) + q_bias).astype(jnp.bfloat16)
    send_q = jnp.take(
        unit_layout(query_rows, part_count, slice_rows, head_count, head_dim), placing, axis=1
    )
    send_g = jnp.take(
        unit_layout(grad_out[0], part_count, slice_rows, head_count, head_dim), placing, axis=1
    )
    send_q = send_q.reshape(slice_rows, devices, 2, head_dim)
    send_g = send_g.reshape(slice_rows, devices, 2, head_dim)
    got_q, got_g = (
        lax.all_to_all(send_q, "seq", split_axis=1, concat_axis=0, tiled=True),
        lax.all_to_all(send_g, "seq", split_axis=1, concat_axis=0, tiled=True),
    )
    got_q = got_q.reshape(tile_count, tile_rows, 2, head_dim)
    got_g = got_g.reshape(tile_count, tile_rows, 2, head_dim)
    copies = devices // kv_count
    send_k = jnp.repeat(k_lin[0].reshape(tok_rows, kv_count, head_dim), copies, axis=1)
    send_v = jnp.repeat(value_projection[0].reshape(tok_rows, kv_count, head_dim), copies, axis=1)
    got_k, got_v = (
        lax.all_to_all(send_k, "seq", split_axis=1, concat_axis=0, tiled=True),
        lax.all_to_all(send_v, "seq", split_axis=1, concat_axis=0, tiled=True),
    )
    key_blocks = got_k.reshape(qblock_count, block_rows, head_dim)
    value_blocks = got_v.reshape(qblock_count, block_rows, head_dim)
    my_units = lax.dynamic_slice_in_dim(placing, 2 * my_index, 2)
    head_of = my_units // part_count
    part_of = my_units % part_count
    tile_ids = jnp.arange(tile_count, dtype=jnp.int32)

    def tables(member):
        first_row = (
            tile_ids // per_slice * tok_rows
            + part_of[member] * slice_rows
            + tile_ids % per_slice * tile_rows
        )
        block_ids = first_row // block_rows
        head_lists = lax.dynamic_index_in_dim(block_lists, head_of[member], 0, keepdims=False)
        head_counts = lax.dynamic_index_in_dim(block_counts, head_of[member], 0, keepdims=False)
        return (jnp.take(head_lists, block_ids, axis=0), jnp.take(head_counts, block_ids, axis=0))

    if joined:
        chosen, counts = tables(0)
        both_q = jnp.concatenate([got_q[:, :, 0], got_q[:, :, 1]], axis=1)
        both_g = jnp.concatenate([got_g[:, :, 0], got_g[:, :, 1]], axis=1)
        grad_both, key_total, value_total = tile_pass(
            both_q, both_g, chosen, counts, key_blocks, value_blocks, scaling
        )
        unit_grads = [grad_both[:, :tile_rows], grad_both[:, tile_rows:]]
    else:
        unit_grads = []
        key_total = None
        value_total = None
        for member in range(2):
            chosen, counts = tables(member)
            grad_one, key_part, value_part = tile_pass(
                got_q[:, :, member],
                got_g[:, :, member],
                chosen,
                counts,
                key_blocks,
                value_blocks,
                scaling,
            )
            unit_grads.append(grad_one)
            key_total = key_part if key_total is None else key_total + key_part
            value_total = value_part if value_total is None else value_total + value_part
    unit_sums = jnp.stack([jnp.sum(grad_one, axis=(0, 1)) for grad_one in unit_grads])
    unit_selector = (my_units[:, None] == jnp.arange(unit_count, dtype=jnp.int32)[None, :]).astype(
        jnp.float32
    )
    bias_parts = jnp.einsum(
        "mu,md->ud",
        unit_selector,
        unit_sums,
        precision=lax.Precision.HIGHEST,
        preferred_element_type=jnp.float32,
    )
    bias_total = lax.psum(bias_parts, ("seq", "rep"))
    dq_send = jnp.stack(unit_grads, axis=2).astype(jnp.bfloat16)
    back_q = lax.all_to_all(dq_send, "seq", split_axis=0, concat_axis=0, tiled=True)
    back_k, back_v = (
        lax.all_to_all(key_total, "seq", split_axis=0, concat_axis=0, tiled=True),
        lax.all_to_all(value_total, "seq", split_axis=0, concat_axis=0, tiled=True),
    )
    arrived = jnp.transpose(back_q, (0, 2, 1, 3)).reshape(unit_count, slice_rows, head_dim)
    unit_ids = jnp.arange(unit_count, dtype=jnp.int32)
    inverse = jnp.sum(
        jnp.where(placing[:, None] == unit_ids[None, :], unit_ids[:, None], 0), axis=0
    )
    by_unit = jnp.take(arrived, inverse, axis=0).reshape(
        head_count, part_count, slice_rows, head_dim
    )
    dq_out = jnp.transpose(by_unit, (1, 2, 0, 3)).reshape(1, tok_rows, head_count * head_dim)
    dk_sum = jnp.sum(back_k.reshape(kv_count, copies, tok_rows, head_dim), axis=1)
    dv_sum = jnp.sum(back_v.reshape(kv_count, copies, tok_rows, head_dim), axis=1)
    dk_out = (
        jnp.transpose(dk_sum, (1, 0, 2))
        .reshape(1, tok_rows, kv_count * head_dim)
        .astype(jnp.bfloat16)
    )
    dv_out = (
        jnp.transpose(dv_sum, (1, 0, 2))
        .reshape(1, tok_rows, kv_count * head_dim)
        .astype(jnp.bfloat16)
    )
    bias_out = jnp.sum(bias_total.reshape(head_count, part_count, head_dim), axis=1).reshape(
        head_count * head_dim
    )
    return (dq_out, dk_out, dv_out, bias_out)


def solution(mesh):
    placed = (
        P("rep", "seq", None),
        P("rep", "seq", None),
        P("rep", "seq", None),
        P("rep", "seq", None),
        P(),
        P(),
        P(),
    )
    return jax.shard_map(
        body,
        mesh=mesh,
        in_specs=placed,
        out_specs=(P("rep", "seq", None), P("rep", "seq", None), P("rep", "seq", None), P()),
        check_vma=False,
    )
```

profile of v0, /device:TPU:0, one launch (start us, length us, event | category | flops | bytes accessed | tf_op | source)
XLA Modules:
  0.0 234.8 jit_solution(10079562226341347012)
XLA Ops:
  0.6 1.0 reshape_squeeze.6
  1.7 0.9 broadcast_in_dim.107
  2.6 8.3 %all-to-all-start.1 = ((bf16[128,16,128]{2,0,1:T(8,128)(2,1)}), bf16[128,16,128]{2,0,1:T(8,128)(2,1)S(1)}, u32[]{:S(2)}, u32[]{:S(2)}) async-start(bf16[128,16,128]{2,0,1:T(8,128)(2,1)} %bitcast.10), calls=%async_computation.1 | async-start | bytes 1048576 | tf_op jit(solution)/shard_map/all_to_all | solution.py:110
  11.0 15.0 %all-to-all-done.1 = bf16[128,16,128]{2,0,1:T(8,128)(2,1)S(1)} async-done(((bf16[128,16,128]{2,0,1:T(8,128)(2,1)}), bf16[128,16,128]{2,0,1:T(8,128)(2,1)S(1)}, u32[]{:S(2)}, u32[]{:S(2)}) %all-to-all-start.1) | async-done | bytes 524320 | tf_op jit(solution)/shard_map/all_to_all | solution.py:110
  26.0 0.9 broadcast_in_dim.109
  26.9 3.9 %all-to-all-start.3 = ((bf16[128,16,128]{2,0,1:T(8,128)(2,1)}), bf16[128,16,128]{2,0,1:T(8,128)(2,1)S(1)}, u32[]{:S(2)}, u32[]{:S(2)}) async-start(bf16[128,16,128]{2,0,1:T(8,128)(2,1)} %bitcast.23), calls=%async_computation.3 | async-start | bytes 1048576 | tf_op jit(solution)/shard_map/all_to_all | solution.py:111
  30.9 1.3 copy.166
  32.2 1.5 copy.167
  33.7 2.3 copy.172
  35.9 2.3 copy.173
  38.2 1.2 add_convert_fusion
  39.4 2.0 gather_fusion.2
  41.4 2.0 gather_fusion.5
  43.4 1.6 broadcast_select_fusion.1
  45.0 0.3 all-to-all-done.3
  45.3 6.8 %all-to-all-start = ((bf16[128,16,2,128]{3,0,2,1:T(8,128)(2,1)}), bf16[128,16,2,128]{3,0,2,1:T(8,128)(2,1)S(1)}, u32[]{:S(2)}, u32[]{:S(2)}) async-start(bf16[128,16,2,128]{3,0,2,1:T(8,128)(2,1)} %bitcast.156), calls=%async_computation | async-start | bytes 2097152 | tf_op jit(solution)/shard_map/all_to_all | solution.py:101
  52.2 0.6 fusion.62
  57.1 0.6 gather_fusion.3
  57.7 0.6 gather_fusion.8
  58.4 16.8 %all-to-all-done = bf16[128,16,2,128]{3,0,2,1:T(8,128)(2,1)S(1)} async-done(((bf16[128,16,2,128]{3,0,2,1:T(8,128)(2,1)}), bf16[128,16,2,128]{3,0,2,1:T(8,128)(2,1)S(1)}, u32[]{:S(2)}, u32[]{:S(2)}) %all-to-all-start) | async-done | bytes 1048608 | tf_op jit(solution)/shard_map/all_to_all | solution.py:101
  75.2 6.0 %all-to-all-start.2 = ((bf16[128,16,2,128]{3,0,2,1:T(8,128)(2,1)}), bf16[128,16,2,128]{3,0,2,1:T(8,128)(2,1)S(1)}, u32[]{:S(2)}, u32[]{:S(2)}) async-start(bf16[128,16,2,128]{3,0,2,1:T(8,128)(2,1)} %bitcast.18), calls=%async_computation.2 | async-start | bytes 2097152 | tf_op jit(solution)/shard_map/all_to_all | solution.py:102
  81.5 0.7 gather_fusion.7
  82.2 0.7 gather_fusion.1
  83.3 1.7 gather_fusion.9
  84.9 1.7 gather_fusion.10
  86.6 1.7 gather_fusion.6
  88.3 1.7 gather_fusion.4
  90.0 4.6 %broadcast_select_fusion.3 = (bf16[16,2,128,128]{3,2,1,0:T(8,128)(2,1)}, bf16[16,2,128,128]{3,2,1,0:T(8,128)(2,1)}, bf16[16,2,128,128]{3,2,1,0:T(8,128)(2,1)}, bf16[16,2,128,128]{3,2,1,0:T(8,128)(2,1)}) fusion(bf16[16,2,128,128]{3,2,1,0:T(8,128)(2,1)} %bitcast.168, pred[16,2]{1,0:T(8,128)(4,1)S(1)} %get-tuple-element.44, ...), kind=kLoop, calls=%fused_computation.57 | loop fusion | flops 2097152 | bytes 8388672 | tf_op jit(solution)/shard_map/jit(_take)/select_n | solution.py:20
  94.7 3.4 %fusion.63 = (f32[16,128]{1,0:T(8,128)S(1)}, f32[16,128,256]{2,1,0:T(8,128)}) fusion(pred[16,256]{1,0:T(8,128)(4,1)S(1)} %bitcast.192, bf16[16,256,128]{2,1,0:T(8,128)(2,1)} %bitcast.166, bf16[16,128,2,128]{3,1,0,2:T(8,128)(2,1)S(1)} %bitcast.157), kind=kOutput, calls=%fused_computation.132 | convolution fusion | flops 136315136 | bytes 3682304 | tf_op jit(solution)/shard_map/sub | solution.py:34
  98.1 5.9 %all-to-all-done.2 = bf16[128,16,2,128]{3,0,2,1:T(8,128)(2,1)S(1)} async-done(((bf16[128,16,2,128]{3,0,2,1:T(8,128)(2,1)}), bf16[128,16,2,128]{3,0,2,1:T(8,128)(2,1)S(1)}, u32[]{:S(2)}, u32[]{:S(2)}) %all-to-all-start.2) | async-done | bytes 1048608 | tf_op jit(solution)/shard_map/all_to_all | solution.py:102
  104.1 2.7 %fusion.19 = f32[16,128]{1,0:T(8,128)S(1)} fusion(bf16[16,256,128]{2,1,0:T(8,128)(2,1)S(1)} %bitcast.182, bf16[16,128,2,128]{3,1,0,2:T(8,128)(2,1)S(1)} %bitcast.174, f32[16,128,256]{2,1,0:T(8,128)} %get-tuple-element.51, f32[16,128]{1,0:T(8,128)S(1)} %get-tuple-element.50), kind=kOutput, calls=%fused_computation.39 | convolution fusion | flops 136050688 | bytes 3686400 | tf_op jit(solution)/shard_map/tqk,tkd->tqd/dot_general | solution.py:36
  107.0 0.8 multiply_convert_fusion
  107.8 0.4 copy-done.2
  108.3 1.3 fusion.61
  109.5 2.2 fusion.64
  111.7 2.8 %fusion.18 = f32[16,128]{1,0:T(8,128)S(1)} fusion(bf16[16,256,128]{2,1,0:T(8,128)(2,1)} %bitcast.180, bf16[16,128,2,128]{3,1,0,2:T(8,128)(2,1)} %bitcast.176, f32[16,128,256]{2,1,0:T(8,128)} %get-tuple-element.53, f32[16,128]{1,0:T(8,128)S(1)} %get-tuple-element.52), kind=kOutput, calls=%fused_computation.38 | convolution fusion | flops 136050688 | bytes 3686400 | tf_op jit(solution)/shard_map/tqk,tkd->tqd/dot_general | solution.py:36
  114.5 0.5 copy-done.16
  115.0 0.8 multiply_convert_fusion.1
  115.8 0.4 copy-done.1
  116.3 0.5 fusion.60
  116.7 0.6 copy-done.3
  117.4 1.0 copy.182
  118.4 6.1 %all-to-all-start.4 = ((bf16[16,128,2,128]{3,1,2,0:T(8,128)(2,1)}), bf16[16,128,2,128]{3,1,2,0:T(8,128)(2,1)}, u32[]{:S(2)}, u32[]{:S(2)}) async-start(bf16[16,128,2,128]{3,1,2,0:T(8,128)(2,1)} %copy.182), calls=%async_computation.4 | async-start | bytes 2097152 | tf_op jit(solution)/shard_map/all_to_all | solution.py:170
  124.7 0.5 convolution_multiply_fusion
  125.2 2.0 fusion.6
  127.2 0.5 convolution_multiply_fusion.1
  127.7 2.0 fusion.12
  129.7 1.3 copy.188
  131.1 16.4 %all-to-all-done.4 = bf16[16,128,2,128]{3,1,2,0:T(8,128)(2,1)} async-done(((bf16[16,128,2,128]{3,1,2,0:T(8,128)(2,1)}), bf16[16,128,2,128]{3,1,2,0:T(8,128)(2,1)}, u32[]{:S(2)}, u32[]{:S(2)}) %all-to-all-start.4) | async-done | bytes 1048608 | tf_op jit(solution)/shard_map/all_to_all | solution.py:170
  147.5 6.1 %all-to-all-start.5 = ((f32[16,128,128]{2,1,0:T(8,128)}), f32[16,128,128]{2,1,0:T(8,128)S(1)}, u32[]{:S(2)}, u32[]{:S(2)}) async-start(f32[16,128,128]{2,1,0:T(8,128)} %copy.188), calls=%async_computation.5 | async-start | bytes 2097152 | tf_op jit(solution)/shard_map/all_to_all | solution.py:172
  153.6 2.5 %fusion.32 = f32[16,256,128]{2,1,0:T(8,128)S(1)} fusion(bf16[16,128,2,128]{3,1,0,2:T(8,128)(2,1)S(1)} %bitcast.178, f32[16,128,256]{2,1,0:T(8,128)} %get-tuple-element.51, f32[16,128]{1,0:T(8,128)S(1)} %get-tuple-element.50), kind=kOutput, calls=%fused_computation.73 | convolution fusion | flops 135266304 | bytes 4726784 | tf_op jit(solution)/shard_map/tqk,tqd->tkd/dot_general | solution.py:50
  156.0 2.0 fusion.2
  158.1 0.9 fusion.31
  158.9 2.0 fusion.15
  161.0 1.3 copy.194
  162.3 14.8 %all-to-all-done.5 = f32[16,128,128]{2,1,0:T(8,128)S(1)} async-done(((f32[16,128,128]{2,1,0:T(8,128)}), f32[16,128,128]{2,1,0:T(8,128)S(1)}, u32[]{:S(2)}, u32[]{:S(2)}) %all-to-all-start.5) | async-done | bytes 1048608 | tf_op jit(solution)/shard_map/all_to_all | solution.py:172
  177.1 5.9 %all-to-all-start.6 = ((f32[16,128,128]{2,1,0:T(8,128)}), f32[16,128,128]{2,1,0:T(8,128)}, u32[]{:S(2)}, u32[]{:S(2)}) async-start(f32[16,128,128]{2,1,0:T(8,128)} %copy.194), calls=%async_computation.6 | async-start | bytes 2097152 | tf_op jit(solution)/shard_map/all_to_all | solution.py:173
  183.3 44.2 %psum.7 = f32[4096]{0:T(1024)} all-reduce(f32[4096]{0:T(1024)S(1)} %convolution_bitcast_fusion), channel_id=1, replica_groups=mesh['seq'=16,'rep'=2] {'seq','rep'}, use_global_device_ids=true, to_apply=%region_11.16 | all-reduce | flops 4096 | bytes 32768 | tf_op jit(solution)/shard_map/psum | solution.py:168
  227.5 2.0 gather_fusion
  229.7 0.7 copy.183
  230.3 1.3 copy.196
  231.8 0.8 copy.197
  232.6 1.3 bitcast_reduce_fusion
  234.0 0.8 copy.198
  (78 shorter events, 3.0 us)
Async XLA Ops:
  0.6 10.3 %copy-start.11 = (bf16[1,128,512]{2,1,0:T(8,128)(2,1)S(1)}, bf16[1,128,512]{2,1,0:T(8,128)(2,1)}, u32[]{:S(2)}) copy-start(bf16[1,128,512]{2,1,0:T(8,128)(2,1)} %param.17) | copy-start | bytes 393220
  1.6 29.2 %copy-start.4 = (bf16[1,128,4096]{2,1,0:T(8,128)(2,1)S(1)}, bf16[1,128,4096]{2,1,0:T(8,128)(2,1)}, u32[]{:S(2)}) copy-start(bf16[1,128,4096]{2,1,0:T(8,128)(2,1)} %param.15) | copy-start | bytes 3145732
  2.6 23.4 %all-to-all-start.1 = ((bf16[128,16,128]{2,0,1:T(8,128)(2,1)}), bf16[128,16,128]{2,0,1:T(8,128)(2,1)S(1)}, u32[]{:S(2)}, u32[]{:S(2)}) async-start(bf16[128,16,128]{2,0,1:T(8,128)(2,1)} %bitcast.10), calls=%async_computation.1 | async-start | bytes 1048576 | tf_op jit(solution)/shard_map/all_to_all | solution.py:110
  26.9 18.4 %all-to-all-start.3 = ((bf16[128,16,128]{2,0,1:T(8,128)(2,1)}), bf16[128,16,128]{2,0,1:T(8,128)(2,1)S(1)}, u32[]{:S(2)}, u32[]{:S(2)}) async-start(bf16[128,16,128]{2,0,1:T(8,128)(2,1)} %bitcast.23), calls=%async_computation.3 | async-start | bytes 1048576 | tf_op jit(solution)/shard_map/all_to_all | solution.py:111
  33.7 4.5 %copy-start.14 = (f32[4096]{0:T(1024)S(1)}, f32[4096]{0:T(1024)}, u32[]{:S(2)}) copy-start(f32[4096]{0:T(1024)} %param.19) | copy-start | bytes 49156
  45.0 11.6 %copy-start.12 = (s32[32,16,2]{0,2,1:T(2,128)S(1)}, s32[32,16,2]{0,2,1:T(2,128)}, u32[]{:S(2)}) copy-start(s32[32,16,2]{0,2,1:T(2,128)} %param.20) | copy-start | bytes 12292
  45.3 36.1 %copy-start.13 = (s32[32,16]{0,1:T(8,128)S(1)}, s32[32,16]{0,1:T(8,128)}, u32[]{:S(2)}) copy-start(s32[32,16]{0,1:T(8,128)} %param.21) | copy-start | bytes 6148
  45.3 29.9 %all-to-all-start = ((bf16[128,16,2,128]{3,0,2,1:T(8,128)(2,1)}), bf16[128,16,2,128]{3,0,2,1:T(8,128)(2,1)S(1)}, u32[]{:S(2)}, u32[]{:S(2)}) async-start(bf16[128,16,2,128]{3,0,2,1:T(8,128)(2,1)} %bitcast.156), calls=%async_computation | async-start | bytes 2097152 | tf_op jit(solution)/shard_map/all_to_all | solution.py:101
  75.2 28.8 %all-to-all-start.2 = ((bf16[128,16,2,128]{3,0,2,1:T(8,128)(2,1)}), bf16[128,16,2,128]{3,0,2,1:T(8,128)(2,1)S(1)}, u32[]{:S(2)}, u32[]{:S(2)}) async-start(bf16[128,16,2,128]{3,0,2,1:T(8,128)(2,1)} %bitcast.18), calls=%async_computation.2 | async-start | bytes 2097152 | tf_op jit(solution)/shard_map/all_to_all | solution.py:102
  98.1 6.0 %copy-start.9 = (bf16[16,2,128,128]{3,2,1,0:T(8,128)(2,1)S(1)}, bf16[16,2,128,128]{3,2,1,0:T(8,128)(2,1)}, u32[]{:S(2)}) copy-start(bf16[16,2,128,128]{3,2,1,0:T(8,128)(2,1)} %get-tuple-element.43) | copy-start | bytes 3145732
  104.1 2.7 %copy-start.5 = (bf16[128,16,2,128]{3,0,1,2:T(8,128)(2,1)}, bf16[128,16,2,128]{3,0,1,2:T(8,128)(2,1)S(1)}, u32[]{:S(2)}) copy-start(bf16[128,16,2,128]{3,0,1,2:T(8,128)(2,1)S(1)} %copy.225) | copy-start | bytes 3145732
  104.1 2.7 %copy-start.10 = (bf16[16,2,128,128]{3,2,1,0:T(8,128)(2,1)S(1)}, bf16[16,2,128,128]{3,2,1,0:T(8,128)(2,1)}, u32[]{:S(2)}) copy-start(bf16[16,2,128,128]{3,2,1,0:T(8,128)(2,1)} %get-tuple-element.43) | copy-start | bytes 3145732
  104.1 2.9 %copy-start.15 = (f32[16,128,256]{2,1,0:T(8,128)S(1)}, f32[16,128,256]{2,1,0:T(8,128)}, u32[]{:S(2)}) copy-start(f32[16,128,256]{2,1,0:T(8,128)} %get-tuple-element.51) | copy-start | bytes 6291460
  107.0 1.2 copy-start.2
  108.3 1.3 copy-start
  111.7 2.8 %copy-start.6 = (bf16[128,16,2,128]{3,0,1,2:T(8,128)(2,1)S(1)}, bf16[128,16,2,128]{3,0,1,2:T(8,128)(2,1)}, u32[]{:S(2)}) copy-start(bf16[128,16,2,128]{3,0,1,2:T(8,128)(2,1)} %copy-done.5) | copy-start | bytes 3145732
  111.7 2.8 %copy-start.8 = (bf16[16,2,128,128]{3,2,1,0:T(8,128)(2,1)S(1)}, bf16[16,2,128,128]{3,2,1,0:T(8,128)(2,1)}, u32[]{:S(2)}) copy-start(bf16[16,2,128,128]{3,2,1,0:T(8,128)(2,1)} %get-tuple-element.56) | copy-start | bytes 3145732
  111.7 3.3 %copy-start.16 = (f32[16,128,256]{2,1,0:T(8,128)S(1)}, f32[16,128,256]{2,1,0:T(8,128)}, u32[]{:S(2)}) copy-start(f32[16,128,256]{2,1,0:T(8,128)} %get-tuple-element.53) | copy-start | bytes 6291460
  115.0 1.2 copy-start.1
  116.3 1.0 copy-start.3
  118.4 29.0 %all-to-all-start.4 = ((bf16[16,128,2,128]{3,1,2,0:T(8,128)(2,1)}), bf16[16,128,2,128]{3,1,2,0:T(8,128)(2,1)}, u32[]{:S(2)}, u32[]{:S(2)}) async-start(bf16[16,128,2,128]{3,1,2,0:T(8,128)(2,1)} %copy.182), calls=%async_computation.4 | async-start | bytes 2097152 | tf_op jit(solution)/shard_map/all_to_all | solution.py:170
  129.7 23.8 %copy-start.7 = (bf16[128,16,2,128]{3,0,1,2:T(8,128)(2,1)S(1)}, bf16[128,16,2,128]{3,0,1,2:T(8,128)(2,1)}, u32[]{:S(2)}) copy-start(bf16[128,16,2,128]{3,0,1,2:T(8,128)(2,1)} %copy-done.5) | copy-start | bytes 3145732
  147.5 29.6 %all-to-all-start.5 = ((f32[16,128,128]{2,1,0:T(8,128)}), f32[16,128,128]{2,1,0:T(8,128)S(1)}, u32[]{:S(2)}, u32[]{:S(2)}) async-start(f32[16,128,128]{2,1,0:T(8,128)} %copy.188), calls=%async_computation.5 | async-start | bytes 2097152 | tf_op jit(solution)/shard_map/all_to_all | solution.py:172
  156.0 2.0 copy-start.17
  177.1 55.5 %all-to-all-start.6 = ((f32[16,128,128]{2,1,0:T(8,128)}), f32[16,128,128]{2,1,0:T(8,128)}, u32[]{:S(2)}, u32[]{:S(2)}) async-start(f32[16,128,128]{2,1,0:T(8,128)} %copy.194), calls=%async_computation.6 | async-start | bytes 2097152 | tf_op jit(solution)/shard_map/all_to_all | solution.py:173
where the time goes:
time: 236 us; the launch traced here: 235 us
  waiting for transfers between devices  69.1 us (29%)
  blocking collectives  44.2 us (19%)
  starting transfers between devices  43.1 us (18%)
  local copies, waits for them, and re-layouts  36.9 us (16%)
  matrix products  27 us (11%)
  other arithmetic  9.45 us (4%)
  between operations  5.06 us (2%)
    psum x1, blocking collectives, body(): bias_total = lax.psum(bias_parts, ('seq', 'rep'))  44.2 us
    all_to_all x1, waiting for transfers between devices, body(): lax.all_to_all(send_q, 'seq', split_axis=1, concat_axis=0, tiled=True)  16.8 us
    all_to_all x1, waiting for transfers between devices, body(): lax.all_to_all(dq_send, 'seq', split_axis=0, concat_axis=0, tiled=True)  16.4 us
    all_to_all x1, waiting for transfers between devices, body(): lax.all_to_all(send_k, 'seq', split_axis=1, concat_axis=0, tiled=True)  15 us
    all_to_all x1, waiting for transfers between devices, body(): lax.all_to_all(key_total, 'seq', split_axis=0, concat_axis=0, tiled=True)  14.8 us
    unnamed x43, local copies, waits for them, and re-layouts  8.7 us
    all_to_all x1, starting transfers between devices, body(): lax.all_to_all(send_k, 'seq', split_axis=1, concat_axis=0, tiled=True)  8.34 us
    all_to_all x1, starting transfers between devices, body(): lax.all_to_all(send_q, 'seq', split_axis=1, concat_axis=0, tiled=True)  6.78 us
  transfers between devices with their start and end apart: 7, of which 6 were waited for; matrix products, arithmetic and copies ran while one was open for 23% of the time, Pallas kernels for 0%

commit v1 on v0

v1 whole, which is shorter than its diff:
```python
import functools

import jax
import jax.numpy as jnp
from jax import lax
from jax.experimental import pallas as pl
from jax.experimental.pallas import tpu as pltpu
from jax.sharding import PartitionSpec as P

NT = (((1,), (1,)), ((), ()))
TN = (((0,), (0,)), ((), ()))
NN = (((1,), (0,)), ((), ()))


def dot(a, b, dims):
    return lax.dot_general(a, b, dims, preferred_element_type=jnp.float32)


def attend_kernel(
    head_dim, group, scaling,
    other_ref, count_ref,
    q_ref, g_ref, bias_ref, k_ref, v_ref, kall_ref, vall_ref,
    dq_ref, part_k_ref, part_v_ref, own_k_ref, own_v_ref, dbq_ref,
    acc_k, acc_v,
):
    step = pl.program_id(0)
    acc_k[...] = jnp.zeros_like(acc_k)
    acc_v[...] = jnp.zeros_like(acc_v)
    own_k_ref[...] = jnp.zeros_like(own_k_ref)
    own_v_ref[...] = jnp.zeros_like(own_v_ref)
    for member in range(group):
        head = step * group + member
        columns = slice(member * head_dim, (member + 1) * head_dim)
        count = count_ref[head]
        other = other_ref[head]

        def finish(queries, grad_q):
            dq_ref[:, columns] = grad_q.astype(jnp.bfloat16)
            dbq_ref[:, columns] = jnp.sum(grad_q, axis=0, keepdims=True)

        def rows():
            queries = (q_ref[:, columns].astype(jnp.float32) + bias_ref[:, columns]).astype(
                jnp.bfloat16
            )
            return queries, g_ref[:, columns]

        @pl.when(count == 1)
        def _():
            queries, grads = rows()
            keys, values = k_ref[...], v_ref[...]
            scores = dot(keys, queries, NT) * scaling
            weights = jnp.exp(scores - jnp.max(scores, axis=0, keepdims=True))
            weights = weights / jnp.sum(weights, axis=0, keepdims=True)
            half = weights.astype(jnp.bfloat16)
            weight_grads = dot(values, grads, NT)
            row_dots = jnp.sum(half.astype(jnp.float32) * weight_grads, axis=0, keepdims=True)
            score_grads = (weights * (weight_grads - row_dots)).astype(jnp.bfloat16)
            finish(queries, scaling * dot(score_grads, keys, TN))
            own_k_ref[...] += dot(score_grads, queries, NN)
            own_v_ref[...] += dot(half, grads, NN)

        @pl.when(count != 1)
        def _():
            queries, grads = rows()
            keys = [k_ref[...], kall_ref[other]]
            values = [v_ref[...], vall_ref[other]]
            scores = [dot(one, queries, NT) * scaling for one in keys]
            top = jnp.maximum(
                jnp.max(scores[0], axis=0, keepdims=True), jnp.max(scores[1], axis=0, keepdims=True)
            )
            weights = [jnp.exp(one - top) for one in scores]
            total = jnp.sum(weights[0], axis=0, keepdims=True) + jnp.sum(
                weights[1], axis=0, keepdims=True
            )
            weights = [one / total for one in weights]
            half = [one.astype(jnp.bfloat16) for one in weights]
            weight_grads = [dot(one, grads, NT) for one in values]
            row_dots = sum(
                jnp.sum(a.astype(jnp.float32) * b, axis=0, keepdims=True)
                for a, b in zip(half, weight_grads)
            )
            score_grads = [
                (a * (b - row_dots)).astype(jnp.bfloat16) for a, b in zip(weights, weight_grads)
            ]
            finish(
                queries,
                scaling * (dot(score_grads[0], keys[0], TN) + dot(score_grads[1], keys[1], TN)),
            )
            own_k_ref[...] += dot(score_grads[0], queries, NN)
            own_v_ref[...] += dot(half[0], grads, NN)
            acc_k[other] += dot(score_grads[1], queries, NN)
            acc_v[other] += dot(half[1], grads, NN)

    own_k_ref[...] = own_k_ref[...] * scaling
    part_k_ref[...] = (acc_k[...] * scaling).astype(jnp.bfloat16)
    part_v_ref[...] = acc_v[...].astype(jnp.bfloat16)


def attend(q, g, bias, k, v, kall, vall, other, count):
    rows, width = q.shape
    blocks = kall.shape[0]
    heads = other.shape[0]
    head_dim = width // heads
    kv_count = k.shape[1] // head_dim
    group = heads // kv_count
    wide = pl.BlockSpec((rows, group * head_dim), lambda s, *_: (0, s))
    thin = pl.BlockSpec((rows, head_dim), lambda s, *_: (0, s))
    line = pl.BlockSpec((1, group * head_dim), lambda s, *_: (0, s))
    whole = pl.BlockSpec((blocks, rows, head_dim), lambda s, *_: (0, 0, s))
    return pl.pallas_call(
        functools.partial(attend_kernel, head_dim, group, head_dim ** (-0.5)),
        grid_spec=pltpu.PrefetchScalarGridSpec(
            num_scalar_prefetch=2,
            grid=(kv_count,),
            in_specs=[wide, wide, line, thin, thin, whole, whole],
            out_specs=[wide, whole, whole, thin, thin, line],
            scratch_shapes=[
                pltpu.VMEM((blocks, rows, head_dim), jnp.float32),
                pltpu.VMEM((blocks, rows, head_dim), jnp.float32),
            ],
        ),
        out_shape=[
            jax.ShapeDtypeStruct((rows, width), jnp.bfloat16),
            jax.ShapeDtypeStruct(kall.shape, jnp.bfloat16),
            jax.ShapeDtypeStruct(vall.shape, jnp.bfloat16),
            jax.ShapeDtypeStruct(k.shape, jnp.float32),
            jax.ShapeDtypeStruct(v.shape, jnp.float32),
            jax.ShapeDtypeStruct((1, width), jnp.float32),
        ],
        compiler_params=pltpu.CompilerParams(vmem_limit_bytes=56 * 1024 * 1024),
        name="attend",
    )(other, count, q, g, bias, k, v, kall, vall)


def body(q_lin, k_lin, value_projection, grad_out, q_bias, block_lists, block_counts):
    me = lax.axis_index("seq")
    assert block_lists.shape[1] == lax.axis_size("seq") and block_lists.shape[2] == 2
    lists = lax.dynamic_index_in_dim(block_lists, me, 1, keepdims=False)
    count = lax.dynamic_index_in_dim(block_counts, me, 1, keepdims=False)
    other = jnp.clip(lists[:, 1], 0, block_lists.shape[1] - 1)
    kall = lax.all_gather(k_lin[0], "seq", axis=0)
    vall = lax.all_gather(value_projection[0], "seq", axis=0)
    dq, part_k, part_v, own_k, own_v, dbq = attend(
        q_lin[0], grad_out[0], q_bias[None], k_lin[0], value_projection[0], kall, vall, other, count
    )
    dbq = lax.psum(dbq[0], ("seq", "rep"))
    sum_k = lax.psum_scatter(part_k, "seq", scatter_dimension=0)
    sum_v = lax.psum_scatter(part_v, "seq", scatter_dimension=0)
    dk = (own_k + sum_k.astype(jnp.float32)).astype(jnp.bfloat16)
    dv = (own_v + sum_v.astype(jnp.float32)).astype(jnp.bfloat16)
    return (dq[None], dk[None], dv[None], dbq)


def solution(mesh):
    placed = (P("rep", "seq", None),) * 4 + (P(),) * 3
    return jax.shard_map(
        body,
        mesh=mesh,
        in_specs=placed,
        out_specs=(P("rep", "seq", None),) * 3 + (P(),),
        check_vma=False,
    )
```

time: 236 us -> 325 us (1.38)
  waiting for transfers between devices: 69.1 us -> 245 us
  starting transfers between devices: 43.1 us -> 0.16 us
  local copies, waits for them, and re-layouts: 36.9 us -> 0.11 us
  matrix products: 27 us -> 0 us
  Pallas kernels: 0 us -> 19.7 us
  between operations: 5.06 us -> 13.8 us
  other arithmetic: 9.45 us -> 4.38 us
    all_gather x0 -> x2, waiting for transfers between devices: none -> 126 us  [the longest x1 63.9 us: body(): kall = lax.all_gather(k_lin[0], 'seq', axis=0)]
    reduce_scatter x0 -> x2, waiting for transfers between devices: none -> 118 us  [the longest x1 78.5 us: body(): sum_v = lax.psum_scatter(part_v, 'seq', scatter_dimension=0)]
    all_to_all x7 -> x0, waiting for transfers between devices: 69.1 us -> none  [the longest x1 16.8 us: body(): lax.all_to_all(send_q, 'seq', split_axis=1, concat_axis=0, tiled=True)]
    all_to_all x7 -> x0, starting transfers between devices: 43.1 us -> none  [the longest x1 8.34 us: body(): lax.all_to_all(send_k, 'seq', split_axis=1, concat_axis=0, tiled=True)]
    dot_general x15 -> x0, matrix products: 21.4 us -> none  [the longest x2 5.44 us: tile_pass(): jnp.einsum('tqk,tkd->tqd', weights_half, value_tiles, preferred_element_t...]
    pallas_call x0 -> x1, Pallas kernels: none -> 19.7 us  [attend(): pl.pallas_call(functools.partial(attend_kernel, head_dim, group, head_dim...]
    gather x11 -> x0, local copies, waits for them, and re-layouts: 15 us -> none  [the longest x2 3.36 us: tile_pass(): jnp.take(value_blocks, chosen, axis=0)]
    unnamed x43 -> x8, local copies, waits for them, and re-layouts: 8.7 us -> 0.11 us
  transfers between devices with their start and end apart: 7 -> 4, of which waited for: 6 -> 4; matrix products, arithmetic and copies ran while one was open for 23% -> 1% of each run, Pallas kernels for 0% -> 0%
where the time goes in v1:
time: 325 us
  waiting for transfers between devices  245 us (75%)
  blocking collectives  41 us (13%)
  Pallas kernels  19.7 us (6%)
  between operations  13.8 us (4%)
  other arithmetic  4.38 us (1%)
    reduce_scatter x1, waiting for transfers between devices, body(): sum_v = lax.psum_scatter(part_v, 'seq', scatter_dimension=0)  78.5 us
    all_gather x1, waiting for transfers between devices, body(): kall = lax.all_gather(k_lin[0], 'seq', axis=0)  63.9 us
    all_gather x1, waiting for transfers between devices, body(): vall = lax.all_gather(value_projection[0], 'seq', axis=0)  62 us
    psum x1, blocking collectives, body(): dbq = lax.psum(dbq[0], ('seq', 'rep'))  41 us
    reduce_scatter x1, waiting for transfers between devices, body(): sum_k = lax.psum_scatter(part_k, 'seq', scatter_dimension=0)  39.1 us
    pallas_call x1, Pallas kernels, attend(): pl.pallas_call(functools.partial(attend_kernel, head_dim, group, head_dim...  19.7 us
  transfers between devices with their start and end apart: 4, of which 4 were waited for; matrix products, arithmetic and copies ran while one was open for 1% of the time, Pallas kernels for 0%

profile of v1, /device:TPU:0, one launch (start us, length us, event | category | flops | bytes accessed | tf_op | source)
XLA Modules:
  0.0 324.6 jit_solution(6628656764558595341)
XLA Ops:
  7.2 0.0 copy-start
  7.2 0.0 all-gather.3.cloned.1.call-start
  7.2 0.7 all-gather.3.cloned.1.call-update
  7.9 0.0 all-gather.5.cloned.1.call-start
  8.0 0.7 all-gather.5.cloned.1.call-update
  8.7 0.0 reduce-scatter.3.cloned.1.call-start
  8.7 0.0 copy-done
  8.7 1.2 dynamic-slice_bitcast_fusion.1
  10.0 63.9 %all-gather.3.cloned.1.call-done.kall_ref = bf16[16,128,512]{2,1,0:T(8,128)(2,1)} async-done(((bf16[1,128,512]{2,1,0:T(8,128)(2,1)}), bf16[16,128,512]{2,1,0:T(8,128)(2,1)}) %all-gather.3.cloned.1.call-update) | async-done | bytes 2097168 | tf_op jit(solution)/shard_map/all_gather | solution.py:141
  73.9 62.0 %all-gather.5.cloned.1.call-done.vall_ref = bf16[16,128,512]{2,1,0:T(8,128)(2,1)} async-done(((bf16[1,128,512]{2,1,0:T(8,128)(2,1)}), bf16[16,128,512]{2,1,0:T(8,128)(2,1)}) %all-gather.5.cloned.1.call-update) | async-done | bytes 2097168 | tf_op jit(solution)/shard_map/all_gather | solution.py:142
  135.9 19.7 %attend.1 = (bf16[128,4096]{1,0:T(8,128)(2,1)}, bf16[16,128,512]{2,1,0:T(8,128)(2,1)}, bf16[16,128,512]{2,1,0:T(8,128)(2,1)}, f32[128,512]{1,0:T(8,128)}, f32[128,512]{1,0:T(8,128)}, /*index=5*/f32[1,4096]{1,0:T(1,128)}) custom-call(s32[32]{0:T(128)} %get-tuple-element.17.other_ref, s32[32]{0:T(128)} %get-tuple-element.16.count_ref, ...), custom_call_target="tpu_custom_call" | custom-call | tf_op jit(solution)/shard_map/attend/pallas_call | solution.py:110
  155.6 0.0 copy-start.3
  155.6 0.0 copy-start.2
  155.6 0.0 copy-start.1
  155.6 0.0 reduce-scatter.3.cloned.1.call-update
  155.6 0.0 reduce-scatter.5.cloned.1.call-start
  155.7 0.5 reduce-scatter.5.cloned.1.call-update
  156.2 0.1 copy-done.3
  156.3 41.0 %psum.7 = f32[4096]{0:T(1024)} all-reduce(f32[4096]{0:T(1024)S(1)} %bitcast.28), channel_id=1, replica_groups=mesh['seq'=16,'rep'=2] {'seq','rep'}, use_global_device_ids=true, to_apply=%region_2.3 | all-reduce | flops 4096 | bytes 32768 | tf_op jit(solution)/shard_map/psum | solution.py:146
  197.3 39.1 %reduce-scatter.3.cloned.1.call-done = bf16[1,128,512]{2,1,0:T(8,128)(2,1)} async-done(((bf16[16,128,512]{2,1,0:T(8,128)(2,1)}), bf16[1,128,512]{2,1,0:T(8,128)(2,1)}) %reduce-scatter.3.cloned.1.call-update) | async-done | bytes 131088 | tf_op jit(solution)/shard_map/reduce_scatter | solution.py:147
  236.4 0.0 copy-done.2
  236.4 1.6 fusion.2
  238.0 78.5 %reduce-scatter.5.cloned.1.call-done = bf16[1,128,512]{2,1,0:T(8,128)(2,1)} async-done(((bf16[16,128,512]{2,1,0:T(8,128)(2,1)}), bf16[1,128,512]{2,1,0:T(8,128)(2,1)}) %reduce-scatter.5.cloned.1.call-update) | async-done | bytes 131088 | tf_op jit(solution)/shard_map/reduce_scatter | solution.py:148
  316.5 0.0 copy-done.1
  316.5 1.6 fusion.3
  (1 shorter events, 0.0 us)
Async XLA Ops:
  7.2 1.6 copy-start
  7.2 66.7 %all-gather.3.cloned.1.call-start = ((), (), s32[]{:S(2)}) async-start(), calls=%async_computation.2 | async-start | bytes 2228224 | tf_op jit(solution)/shard_map/all_gather | solution.py:141
  7.9 128.0 %all-gather.5.cloned.1.call-start = ((), (), s32[]{:S(2)}) async-start(), calls=%async_computation.3 | async-start | bytes 2228224 | tf_op jit(solution)/shard_map/all_gather | solution.py:142
  8.7 227.7 %reduce-scatter.3.cloned.1.call-start = ((), (), s32[]{:S(2)}) async-start(), calls=%async_computation.4 | async-start | bytes 2228224 | tf_op jit(solution)/shard_map/reduce_scatter | solution.py:147
  155.6 0.7 copy-start.3
  155.6 80.8 %copy-start.2 = (f32[128,512]{1,0:T(8,128)S(1)}, f32[128,512]{1,0:T(8,128)}, u32[]{:S(2)}) copy-start(f32[128,512]{1,0:T(8,128)} %get-tuple-element.11) | copy-start | bytes 786436
  155.6 160.9 %copy-start.1 = (f32[128,512]{1,0:T(8,128)S(1)}, f32[128,512]{1,0:T(8,128)}, u32[]{:S(2)}) copy-start(f32[128,512]{1,0:T(8,128)} %get-tuple-element.13) | copy-start | bytes 786436
  155.6 160.8 %reduce-scatter.5.cloned.1.call-start = ((), (), s32[]{:S(2)}) async-start(), calls=%async_computation.5 | async-start | bytes 2228224 | tf_op jit(solution)/shard_map/reduce_scatter | solution.py:148
Sparse Core Ops, SparseCore 0:
  10.8 63.0 all-gather.2
  76.7 59.1 all-gather.4
  155.7 80.5 reduce-scatter.2
  238.5 77.9 reduce-scatter.4

commit v2 on v1

--- a/solution.py
+++ b/solution.py
@@ -132,23 +132,249 @@
     )(other, count, q, g, bias, k, v, kall, vall)
 
 
+MESH = pl.DeviceIdType.MESH
+
+
+def place():
+    me = lax.axis_index("seq")
+    n = lax.axis_size("seq")
+    lines = n // 4
+    z, p = me // 4, me % 4
+    x, y = p % 2, p // 2
+    px = y * 2 + (1 - x)
+    py = (1 - y) * 2 + x
+    far = (1 - y) * 2 + (1 - x)
+    return lines, z, p, px, py, far
+
+
+def greet(targets, extra=()):
+    barrier = pltpu.get_barrier_semaphore()
+    for target in targets:
+        pl.semaphore_signal(barrier, inc=1, device_id={"seq": target}, device_id_type=MESH)
+    for target in extra:
+        pl.semaphore_signal(barrier, inc=1, device_id={"rep": target}, device_id_type=MESH)
+    pl.semaphore_wait(barrier, len(targets) + len(extra))
+
+
+class Sender:
+    def __init__(self, send_sem, recv_sem):
+        self.send_sem, self.recv_sem, self.next, self.open = send_sem, recv_sem, 0, []
+
+    def __call__(self, src, dst, **target):
+        copy = pltpu.make_async_remote_copy(
+            src_ref=src,
+            dst_ref=dst,
+            send_sem=self.send_sem.at[self.next],
+            recv_sem=self.recv_sem.at[self.next],
+            device_id=target,
+            device_id_type=MESH,
+        )
+        self.next += 1
+        copy.start()
+        self.open.append(copy)
+        return copy
+
+    def drain(self):
+        for copy in self.open:
+            copy.wait_send()
+
+
+def gather_kernel(k_ref, v_ref, kall_ref, vall_ref, send_sem, recv_sem, local_sem):
+    lines, z, p, px, py, far = place()
+    me = z * 4 + p
+    zs = [lax.rem(z + lines - d, lines) for d in range(lines)]
+    up = [lax.rem(z + d, lines) for d in range(lines)]
+    greet([up[d] * 4 + p for d in range(1, lines)] + [z * 4 + px, z * 4 + py])
+    send = Sender(send_sem, recv_sem)
+    arrays = [(k_ref, kall_ref, px, py), (v_ref, vall_ref, py, px)]
+    along, first, last = {}, {}, []
+    own = []
+    for a, (src, out, f, s) in enumerate(arrays):
+        own.append(pltpu.make_async_copy(src, out.at[me], local_sem.at[a]))
+        own[-1].start()
+    for d in range(1, lines):
+        for a, (src, out, f, s) in enumerate(arrays):
+            along[a, d] = send(src, out.at[me], seq=up[d] * 4 + p)
+    for d in range(lines + 1):
+        if d < lines:
+            for a, (src, out, f, s) in enumerate(arrays):
+                spot = zs[d] * 4 + p
+                if d:
+                    along[a, d].wait_recv()
+                piece = out.at[spot] if d else src
+                first[a, d] = send(piece, out.at[spot], seq=z * 4 + f)
+            for a, (src, out, f, s) in enumerate(arrays):
+                spot = zs[d] * 4 + p
+                piece = out.at[spot] if d else src
+                last.append(send(piece, out.at[spot], seq=z * 4 + s))
+        if d:
+            for a, (src, out, f, s) in enumerate(arrays):
+                spot = zs[d - 1] * 4 + f
+                first[a, d - 1].wait_recv()
+                last.append(send(out.at[spot], out.at[spot], seq=z * 4 + s))
+    for copy in last:
+        copy.wait_recv()
+    send.drain()
+    for copy in own:
+        copy.wait()
+
+
+def gather(k, v):
+    n = lax.axis_size("seq")
+    assert n % 4 == 0
+    copies = 2 * (n // 4 - 1 + 3 * (n // 4))
+    spec = pl.BlockSpec(memory_space=pl.ANY)
+    return pl.pallas_call(
+        gather_kernel,
+        in_specs=[spec, spec],
+        out_specs=[spec, spec],
+        out_shape=[jax.ShapeDtypeStruct((n,) + one.shape, one.dtype) for one in (k, v)],
+        scratch_shapes=[
+            pltpu.SemaphoreType.DMA((copies,)),
+            pltpu.SemaphoreType.DMA((copies,)),
+            pltpu.SemaphoreType.DMA((2,)),
+        ],
+        compiler_params=pltpu.CompilerParams(collective_id=1, has_side_effects=True),
+        name="gather",
+    )(k, v)
+
+
+def scatter_kernel(
+    part_k, part_v, own_k, own_v, bias_ref,
+    dk_ref, dv_ref, dbq_ref,
+    half_k, half_v, line_k, line_v, end_k, end_v,
+    rep_slots, x_slots, y_slots, z_slots, sums, send_sem, recv_sem,
+):
+    lines, z, p, px, py, far = place()
+    me = z * 4 + p
+    reps, rep = lax.axis_size("rep"), lax.axis_index("rep")
+    up = [lax.rem(z + d, lines) for d in range(lines)]
+    others = [lax.rem(rep + d, reps) for d in range(1, reps)]
+    greet([up[d] * 4 + p for d in range(1, lines)] + [z * 4 + px, z * 4 + py], others)
+    send = Sender(send_sem, recv_sem)
+    arrays = [
+        (part_k, own_k, dk_ref, half_k, line_k, end_k, px, py),
+        (part_v, own_v, dv_ref, half_v, line_v, end_v, py, px),
+    ]
+    order = list(range(1, lines)) + [0]
+
+    rep_slots[rep] = bias_ref[...]
+    bias = [send(bias_ref, rep_slots.at[rep], rep=other) for other in others]
+    x, y = p % 2, p // 2
+    near, cross, down, ends = {}, {}, {}, []
+    for d in order:
+        for a, (part, own, out, half, line, end, f, s) in enumerate(arrays):
+            cross[a, d] = send(part.at[up[d] * 4 + far], half.at[d, 1], seq=z * 4 + s)
+        for a, (part, own, out, half, line, end, f, s) in enumerate(arrays):
+            near[a, d] = send(part.at[up[d] * 4 + s], half.at[d, 0], seq=z * 4 + s)
+
+    def total(slots, count):
+        result = slots[0]
+        for j in range(1, count):
+            result = result + slots[j]
+        return result
+
+    def relay(stage):
+        nonlocal bias
+        for copy in bias:
+            copy.wait_recv()
+        if stage == 0:
+            sums[0] = total(rep_slots, reps)
+            x_slots[x] = sums[0]
+            bias = [send(sums.at[0], x_slots.at[x], seq=z * 4 + px)]
+        elif stage == 1:
+            sums[1] = total(x_slots, 2)
+            y_slots[y] = sums[1]
+            bias = [send(sums.at[1], y_slots.at[y], seq=z * 4 + py)]
+        elif stage == 2:
+            sums[2] = total(y_slots, 2)
+            z_slots[z] = sums[2]
+            bias = [
+                send(sums.at[2], z_slots.at[z], seq=up[d] * 4 + p) for d in range(1, lines)
+            ]
+        else:
+            dbq_ref[...] = total(z_slots, lines)
+
+    stage = 0
+    for j in range(lines + 1):
+        if j < lines:
+            d = order[j]
+            for a, (part, own, out, half, line, end, f, s) in enumerate(arrays):
+                cross[a, d].wait_recv()
+                half[d, 1] = half[d, 1] + part[up[d] * 4 + f]
+                down[a, d] = send(half.at[d, 1], line.at[d], seq=z * 4 + f)
+            for a, (part, own, out, half, line, end, f, s) in enumerate(arrays):
+                near[a, d].wait_recv()
+        if stage < 3:
+            relay(stage)
+            stage += 1
+        if j:
+            d = order[j - 1]
+            for a, (part, own, out, half, line, end, f, s) in enumerate(arrays):
+                down[a, d].wait_recv()
+                summed = (
+                    half[d, 0].astype(jnp.float32)
+                    + part[up[d] * 4 + p].astype(jnp.float32)
+                    + line[d].astype(jnp.float32)
+                )
+                if d:
+                    line[d] = summed.astype(jnp.bfloat16)
+                    ends.append((a, d, send(line.at[d], end.at[d - 1], seq=up[d] * 4 + p)))
+                else:
+                    line[d] = summed.astype(jnp.bfloat16)
+    while stage < 4:
+        relay(stage)
+        stage += 1
+    for a, d, copy in ends:
+        copy.wait_recv()
+    for part, own, out, half, line, end, f, s in arrays:
+        result = own[...] + line[0].astype(jnp.float32)
+        for d in range(lines - 1):
+            result = result + end[d].astype(jnp.float32)
+        out[...] = result.astype(jnp.bfloat16)
+    send.drain()
+
+
+def scatter(part_k, part_v, own_k, own_v, bias):
+    n, reps = lax.axis_size("seq"), lax.axis_size("rep")
+    lines = n // 4
+    block, kind = part_k.shape[1:], part_k.dtype
+    copies = 2 * (4 * lines - 1) + (reps - 1) + 2 + (lines - 1)
+    spec = pl.BlockSpec(memory_space=pltpu.VMEM)
+    slots = [reps, 2, 2, lines, 3]
+    return pl.pallas_call(
+        scatter_kernel,
+        in_specs=[spec] * 5,
+        out_specs=[spec] * 3,
+        out_shape=[
+            jax.ShapeDtypeStruct(block, kind),
+            jax.ShapeDtypeStruct(block, kind),
+            jax.ShapeDtypeStruct(bias.shape, jnp.float32),
+        ],
+        scratch_shapes=[pltpu.VMEM((lines, 2) + block, kind)] * 2
+        + [pltpu.VMEM((lines,) + block, kind)] * 2
+        + [pltpu.VMEM((lines - 1,) + block, kind)] * 2
+        + [pltpu.VMEM((count,) + bias.shape, jnp.float32) for count in slots]
+        + [pltpu.SemaphoreType.DMA((copies,))] * 2,
+        compiler_params=pltpu.CompilerParams(
+            collective_id=2, has_side_effects=True, vmem_limit_bytes=60 * 1024 * 1024
+        ),
+        name="scatter",
+    )(part_k, part_v, own_k, own_v, bias)
+
+
 def body(q_lin, k_lin, value_projection, grad_out, q_bias, block_lists, block_counts):
     me = lax.axis_index("seq")
     assert block_lists.shape[1] == lax.axis_size("seq") and block_lists.shape[2] == 2
     lists = lax.dynamic_index_in_dim(block_lists, me, 1, keepdims=False)
     count = lax.dynamic_index_in_dim(block_counts, me, 1, keepdims=False)
     other = jnp.clip(lists[:, 1], 0, block_lists.shape[1] - 1)
-    kall = lax.all_gather(k_lin[0], "seq", axis=0)
-    vall = lax.all_gather(value_projection[0], "seq", axis=0)
+    kall, vall = gather(k_lin[0], value_projection[0])
     dq, part_k, part_v, own_k, own_v, dbq = attend(
         q_lin[0], grad_out[0], q_bias[None], k_lin[0], value_projection[0], kall, vall, other, count
     )
-    dbq = lax.psum(dbq[0], ("seq", "rep"))
-    sum_k = lax.psum_scatter(part_k, "seq", scatter_dimension=0)
-    sum_v = lax.psum_scatter(part_v, "seq", scatter_dimension=0)
-    dk = (own_k + sum_k.astype(jnp.float32)).astype(jnp.bfloat16)
-    dv = (own_v + sum_v.astype(jnp.float32)).astype(jnp.bfloat16)
-    return (dq[None], dk[None], dv[None], dbq)
+    dk, dv, dbq = scatter(part_k, part_v, own_k, own_v, dbq.reshape(8, -1))
+    return (dq[None], dk[None], dv[None], dbq.reshape(-1))
 
 
 def solution(mesh):

time: 325 us -> 135 us (0.42)
  waiting for transfers between devices: 245 us -> 0 us
  Pallas kernels: 19.7 us -> 123 us
  blocking collectives: 41 us -> 0 us
  between operations: 13.8 us -> 0.67 us
  local copies, waits for them, and re-layouts: 0.11 us -> 6.3 us
    all_gather x2 -> x0, waiting for transfers between devices: 126 us -> none  [the longest x1 63.9 us: body(): kall = lax.all_gather(k_lin[0], 'seq', axis=0)]
    reduce_scatter x2 -> x0, waiting for transfers between devices: 118 us -> none  [the longest x1 78.5 us: body(): sum_v = lax.psum_scatter(part_v, 'seq', scatter_dimension=0)]
    pallas_call x0 -> x2, Pallas kernels: none -> 104 us  [the longest x1 58.9 us: scatter(): pl.pallas_call(scatter_kernel, in_specs=[spec] * 5, out_specs=[spec] * 3,...]
    psum x1 -> x0, blocking collectives: 41 us -> none  [body(): dbq = lax.psum(dbq[0], ('seq', 'rep'))]
    unnamed x8 -> x5, local copies, waits for them, and re-layouts: 0.11 us -> 5.17 us
  transfers between devices with their start and end apart: 4 -> 0, of which waited for: 4 -> 0; matrix products, arithmetic and copies ran while one was open for 1% -> 0% of each run, Pallas kernels for 0% -> 0%
where the time goes in v2:
time: 135 us; the launch traced here: 133 us
  Pallas kernels  123 us (91%)
  local copies, waits for them, and re-layouts  6.3 us (5%)
  other arithmetic  2.61 us (2%)
    pallas_call x1, Pallas kernels, scatter(): pl.pallas_call(scatter_kernel, in_specs=[spec] * 5, out_specs=[spec] * 3,...  58.9 us
    pallas_call x1, Pallas kernels, gather(): pl.pallas_call(gather_kernel, in_specs=[spec, spec], out_specs=[spec, spe...  45.4 us
    pallas_call x1, Pallas kernels, attend(): pl.pallas_call(functools.partial(attend_kernel, head_dim, group, head_dim...  19.2 us
    unnamed x5, local copies, waits for them, and re-layouts  5.17 us

profile of v2, /device:TPU:0, one launch (start us, length us, event | category | flops | bytes accessed | tf_op | source)
XLA Modules:
  0.0 133.0 jit_solution(14768712646655234583)
XLA Ops:
  0.6 0.0 copy-start
  0.6 0.7 copy-done
  1.4 1.2 dynamic-slice_bitcast_fusion.1
  2.6 45.4 %gather.1 = (bf16[16,128,512]{2,1,0:T(8,128)(2,1)}, bf16[16,128,512]{2,1,0:T(8,128)(2,1)}) custom-call(bf16[128,512]{1,0:T(8,128)(2,1)} %bitcast.18, bf16[128,512]{1,0:T(8,128)(2,1)} %bitcast.20), custom_call_target="tpu_custom_call" | custom-call | tf_op jit(solution)/shard_map/gather/pallas_call | solution.py:227
  47.9 19.2 %attend.1 = (bf16[128,4096]{1,0:T(8,128)(2,1)}, bf16[16,128,512]{2,1,0:T(8,128)(2,1)}, bf16[16,128,512]{2,1,0:T(8,128)(2,1)}, f32[128,512]{1,0:T(8,128)}, f32[128,512]{1,0:T(8,128)}, /*index=5*/f32[1,4096]{1,0:T(1,128)}) custom-call(s32[32]{0:T(128)} %get-tuple-element.27.other_ref, s32[32]{0:T(128)} %get-tuple-element.26.count_ref, ...), custom_call_target="tpu_custom_call" | custom-call | tf_op jit(solution)/shard_map/attend/pallas_call | solution.py:110
  67.1 0.5 broadcast.7
  67.6 1.4 %reduce.3 = f32[4096]{0:T(1024)S(1)} reduce(f32[1,4096]{1,0:T(1,128)} %get-tuple-element.22, f32[]{:T(128)} %broadcast.7), dimensions={0}, to_apply=%get-tuple-element.22.reduce_sub_computation.3 | reduce | bytes 32772 | tf_op jit(solution)/shard_map/attend/pallas_call | solution.py:110
  69.0 0.6 reshape.17.bias_ref
  69.7 58.9 %scatter.1 = (bf16[128,512]{1,0:T(8,128)(2,1)}, bf16[128,512]{1,0:T(8,128)(2,1)}, f32[8,512]{1,0:T(8,128)}) custom-call(bf16[16,128,512]{2,1,0:T(8,128)(2,1)} %get-tuple-element.18.part_k, bf16[16,128,512]{2,1,0:T(8,128)(2,1)} %get-tuple-element.19.part_v, f32[128,512]{1,0:T(8,128)} %get-tuple-element.20.own_k, f32[128,512]{1,0:T(8,128)} %get-tuple-element.21.own_v, ...), custom_call_target="tpu_custom_call" | custom-call | tf_op jit(solution)/shard_map/scatter/pallas_call | solution.py:345
  128.5 1.3 copy.11
  129.8 1.6 %copy.14 = bf16[1,128,512]{2,1,0:T(8,128)(2,1)} copy(bf16[1,128,512]{2,1,0:T(8,128)(2,1)} %bitcast.23) | data formatting | bytes 262144
  131.4 1.6 %copy.15 = bf16[1,128,512]{2,1,0:T(8,128)(2,1)} copy(bf16[1,128,512]{2,1,0:T(8,128)(2,1)} %bitcast.22) | data formatting | bytes 262144
  (1 shorter events, 0.0 us)
Async XLA Ops:
  0.6 0.7 copy-start

commit v3 on v2

--- a/solution.py
+++ b/solution.py
@@ -26,42 +26,46 @@
     step = pl.program_id(0)
     acc_k[...] = jnp.zeros_like(acc_k)
     acc_v[...] = jnp.zeros_like(acc_v)
-    own_k_ref[...] = jnp.zeros_like(own_k_ref)
-    own_v_ref[...] = jnp.zeros_like(own_v_ref)
+
+    def finish(columns, grad_q):
+        dq_ref[:, columns] = grad_q.astype(jnp.bfloat16)
+        dbq_ref[:, columns] = jnp.sum(grad_q, axis=0, keepdims=True)
+
+    def rows(columns):
+        queries = (q_ref[:, columns].astype(jnp.float32) + bias_ref[:, columns]).astype(
+            jnp.bfloat16
+        )
+        return queries, g_ref[:, columns]
+
+    own_k = own_v = None
+    for member in range(group):
+        columns = slice(member * head_dim, (member + 1) * head_dim)
+        alone = jnp.where(count_ref[step * group + member] == 1, 1.0, 0.0)
+        queries, grads = rows(columns)
+        keys, values = k_ref[...], v_ref[...]
+        scores = dot(keys, queries, NT) * scaling
+        weights = jnp.exp(scores - jnp.max(scores, axis=0, keepdims=True))
+        weights = weights * (alone / jnp.sum(weights, axis=0, keepdims=True))
+        half = weights.astype(jnp.bfloat16)
+        weight_grads = dot(values, grads, NT)
+        row_dots = jnp.sum(half.astype(jnp.float32) * weight_grads, axis=0, keepdims=True)
+        score_grads = (weights * (weight_grads - row_dots)).astype(jnp.bfloat16)
+        finish(columns, scaling * dot(score_grads, keys, TN))
+        more_k, more_v = dot(score_grads, queries, NN), dot(half, grads, NN)
+        own_k = more_k if own_k is None else own_k + more_k
+        own_v = more_v if own_v is None else own_v + more_v
+    own_k_ref[...] = own_k
+    own_v_ref[...] = own_v
+
     for member in range(group):
         head = step * group + member
         columns = slice(member * head_dim, (member + 1) * head_dim)
         count = count_ref[head]
         other = other_ref[head]
 
-        def finish(queries, grad_q):
-            dq_ref[:, columns] = grad_q.astype(jnp.bfloat16)
-            dbq_ref[:, columns] = jnp.sum(grad_q, axis=0, keepdims=True)
-
-        def rows():
-            queries = (q_ref[:, columns].astype(jnp.float32) + bias_ref[:, columns]).astype(
-                jnp.bfloat16
-            )
-            return queries, g_ref[:, columns]
-
-        @pl.when(count == 1)
-        def _():
-            queries, grads = rows()
-            keys, values = k_ref[...], v_ref[...]
-            scores = dot(keys, queries, NT) * scaling
-            weights = jnp.exp(scores - jnp.max(scores, axis=0, keepdims=True))
-            weights = weights / jnp.sum(weights, axis=0, keepdims=True)
-            half = weights.astype(jnp.bfloat16)
-            weight_grads = dot(values, grads, NT)
-            row_dots = jnp.sum(half.astype(jnp.float32) * weight_grads, axis=0, keepdims=True)
-            score_grads = (weights * (weight_grads - row_dots)).astype(jnp.bfloat16)
-            finish(queries, scaling * dot(score_grads, keys, TN))
-            own_k_ref[...] += dot(score_grads, queries, NN)
-            own_v_ref[...] += dot(half, grads, NN)
-
         @pl.when(count != 1)
         def _():
-            queries, grads = rows()
+            queries, grads = rows(columns)
             keys = [k_ref[...], kall_ref[other]]
             values = [v_ref[...], vall_ref[other]]
             scores = [dot(one, queries, NT) * scaling for one in keys]
@@ -72,7 +76,8 @@
             total = jnp.sum(weights[0], axis=0, keepdims=True) + jnp.sum(
                 weights[1], axis=0, keepdims=True
             )
-            weights = [one / total for one in weights]
+            scale_to = 1.0 / total
+            weights = [one * scale_to for one in weights]
             half = [one.astype(jnp.bfloat16) for one in weights]
             weight_grads = [dot(one, grads, NT) for one in values]
             row_dots = sum(
@@ -83,7 +88,7 @@
                 (a * (b - row_dots)).astype(jnp.bfloat16) for a, b in zip(weights, weight_grads)
             ]
             finish(
-                queries,
+                columns,
                 scaling * (dot(score_grads[0], keys[0], TN) + dot(score_grads[1], keys[1], TN)),
             )
             own_k_ref[...] += dot(score_grads[0], queries, NN)
@@ -262,11 +267,17 @@
     bias = [send(bias_ref, rep_slots.at[rep], rep=other) for other in others]
     x, y = p % 2, p // 2
     near, cross, down, ends = {}, {}, {}, []
-    for d in order:
+
+    def open_step(j):
+        if j >= lines:
+            return
+        d = order[j]
         for a, (part, own, out, half, line, end, f, s) in enumerate(arrays):
             cross[a, d] = send(part.at[up[d] * 4 + far], half.at[d, 1], seq=z * 4 + s)
         for a, (part, own, out, half, line, end, f, s) in enumerate(arrays):
             near[a, d] = send(part.at[up[d] * 4 + s], half.at[d, 0], seq=z * 4 + s)
+
+    open_step(0)
 
     def total(slots, count):
         result = slots[0]
@@ -298,6 +309,7 @@
     stage = 0
     for j in range(lines + 1):
         if j < lines:
+            open_step(j + 1)
             d = order[j]
             for a, (part, own, out, half, line, end, f, s) in enumerate(arrays):
                 cross[a, d].wait_recv()
@@ -373,7 +385,7 @@
     dq, part_k, part_v, own_k, own_v, dbq = attend(
         q_lin[0], grad_out[0], q_bias[None], k_lin[0], value_projection[0], kall, vall, other, count
     )
-    dk, dv, dbq = scatter(part_k, part_v, own_k, own_v, dbq.reshape(8, -1))
+    dk, dv, dbq = scatter(part_k, part_v, own_k, own_v, dbq)
     return (dq[None], dk[None], dv[None], dbq.reshape(-1))
 
 

time: 135 us -> 122 us (0.904)
  Pallas kernels: 123 us -> 114 us
  other arithmetic: 2.61 us -> 1.21 us
    pallas_call x1, Pallas kernels: 58.9 us -> 51.2 us  [scatter(): pl.pallas_call(scatter_kernel, in_specs=[spec] * 5, out_specs=[spec] * 3,...]
    pallas_call x1, Pallas kernels: 19.2 us -> 17.3 us  [attend(): pl.pallas_call(functools.partial(attend_kernel, head_dim, group, head_dim...]
    pallas_call x1 -> x0, other arithmetic: 1.4 us -> none  [attend(): pl.pallas_call(functools.partial(attend_kernel, head_dim, group, head_dim...]
where the time goes in v3:
time: 122 us; the launch traced here: 121 us
  Pallas kernels  114 us (93%)
  local copies, waits for them, and re-layouts  5.17 us (4%)
    pallas_call x1, Pallas kernels, scatter(): pl.pallas_call(scatter_kernel, in_specs=[spec] * 5, out_specs=[spec] * 3,...  51.2 us
    pallas_call x1, Pallas kernels, gather(): pl.pallas_call(gather_kernel, in_specs=[spec, spec], out_specs=[spec, spe...  45.4 us
    pallas_call x1, Pallas kernels, attend(): pl.pallas_call(functools.partial(attend_kernel, head_dim, group, head_dim...  17.3 us
    unnamed x5, local copies, waits for them, and re-layouts  5.17 us

profile of v3, /device:TPU:0, one launch (start us, length us, event | category | flops | bytes accessed | tf_op | source)
XLA Modules:
  0.0 120.9 jit_solution(1336702307811274118)
XLA Ops:
  0.6 0.0 copy-start
  0.6 0.7 copy-done
  1.4 1.2 dynamic-slice_bitcast_fusion.1
  2.6 45.4 %gather.1 = (bf16[16,128,512]{2,1,0:T(8,128)(2,1)}, bf16[16,128,512]{2,1,0:T(8,128)(2,1)}) custom-call(bf16[128,512]{1,0:T(8,128)(2,1)} %bitcast.17, bf16[128,512]{1,0:T(8,128)(2,1)} %bitcast.19), custom_call_target="tpu_custom_call" | custom-call | tf_op jit(solution)/shard_map/gather/pallas_call | solution.py:232
  47.9 17.3 %attend.1 = (bf16[128,4096]{1,0:T(8,128)(2,1)}, bf16[16,128,512]{2,1,0:T(8,128)(2,1)}, bf16[16,128,512]{2,1,0:T(8,128)(2,1)}, f32[128,512]{1,0:T(8,128)}, f32[128,512]{1,0:T(8,128)}, /*index=5*/f32[1,4096]{1,0:T(1,128)}) custom-call(s32[32]{0:T(128)} %get-tuple-element.27.other_ref, s32[32]{0:T(128)} %get-tuple-element.26.count_ref, ...), custom_call_target="tpu_custom_call" | custom-call | tf_op jit(solution)/shard_map/attend/pallas_call | solution.py:115
  65.3 51.2 %scatter.1 = (bf16[128,512]{1,0:T(8,128)(2,1)}, bf16[128,512]{1,0:T(8,128)(2,1)}, f32[1,4096]{1,0:T(1,128)}) custom-call(bf16[16,128,512]{2,1,0:T(8,128)(2,1)} %get-tuple-element.18.part_k, bf16[16,128,512]{2,1,0:T(8,128)(2,1)} %get-tuple-element.19.part_v, f32[128,512]{1,0:T(8,128)} %get-tuple-element.20.own_k, f32[128,512]{1,0:T(8,128)} %get-tuple-element.21.own_v, ...), custom_call_target="tpu_custom_call" | custom-call | tf_op jit(solution)/shard_map/scatter/pallas_call | solution.py:357
  116.4 1.6 %copy.14 = bf16[1,128,512]{2,1,0:T(8,128)(2,1)} copy(bf16[1,128,512]{2,1,0:T(8,128)(2,1)} %bitcast.22) | data formatting | bytes 262144
  118.0 1.6 %copy.15 = bf16[1,128,512]{2,1,0:T(8,128)(2,1)} copy(bf16[1,128,512]{2,1,0:T(8,128)(2,1)} %bitcast.21) | data formatting | bytes 262144
  119.6 1.3 %copy.16 = f32[4096]{0:T(1024)} copy(f32[4096]{0:T(1024)} %bitcast.24) | data formatting | bytes 32768
  (1 shorter events, 0.0 us)
Async XLA Ops:
  0.6 0.7 copy-start

commit v4 on v3

--- a/solution.py
+++ b/solution.py
@@ -278,6 +278,7 @@
             near[a, d] = send(part.at[up[d] * 4 + s], half.at[d, 0], seq=z * 4 + s)
 
     open_step(0)
+    open_step(1)
 
     def total(slots, count):
         result = slots[0]
@@ -309,12 +310,12 @@
     stage = 0
     for j in range(lines + 1):
         if j < lines:
-            open_step(j + 1)
             d = order[j]
             for a, (part, own, out, half, line, end, f, s) in enumerate(arrays):
                 cross[a, d].wait_recv()
                 half[d, 1] = half[d, 1] + part[up[d] * 4 + f]
                 down[a, d] = send(half.at[d, 1], line.at[d], seq=z * 4 + f)
+            open_step(j + 2)
             for a, (part, own, out, half, line, end, f, s) in enumerate(arrays):
                 near[a, d].wait_recv()
         if stage < 3:

time: 122 us -> 129 us (1.057)
  the two profiles are of different devices: /device:TPU:0 before, /device:TPU:12 now
where the time goes in v4:
time: 129 us
  Pallas kernels  122 us (95%)
  local copies, waits for them, and re-layouts  5.17 us (4%)
    pallas_call x1, Pallas kernels, scatter(): pl.pallas_call(scatter_kernel, in_specs=[spec] * 5, out_specs=[spec] * 3,...  62.9 us
    pallas_call x1, Pallas kernels, gather(): pl.pallas_call(gather_kernel, in_specs=[spec, spec], out_specs=[spec, spe...  39.7 us
    pallas_call x1, Pallas kernels, attend(): pl.pallas_call(functools.partial(attend_kernel, head_dim, group, head_dim...  19.3 us
    unnamed x5, local copies, waits for them, and re-layouts  5.17 us

profile of v4, /device:TPU:12, one launch (start us, length us, event | category | flops | bytes accessed | tf_op | source)
XLA Modules:
  0.0 129.0 jit_solution(5608211357458676721)
XLA Ops:
  0.6 0.0 copy-start
  0.6 0.7 copy-done
  1.4 1.2 dynamic-slice_bitcast_fusion.1
  2.6 39.7 %gather.1 = (bf16[16,128,512]{2,1,0:T(8,128)(2,1)}, bf16[16,128,512]{2,1,0:T(8,128)(2,1)}) custom-call(bf16[128,512]{1,0:T(8,128)(2,1)} %bitcast.17, bf16[128,512]{1,0:T(8,128)(2,1)} %bitcast.19), custom_call_target="tpu_custom_call" | custom-call | tf_op jit(solution)/shard_map/gather/pallas_call | solution.py:232
  42.3 19.3 %attend.1 = (bf16[128,4096]{1,0:T(8,128)(2,1)}, bf16[16,128,512]{2,1,0:T(8,128)(2,1)}, bf16[16,128,512]{2,1,0:T(8,128)(2,1)}, f32[128,512]{1,0:T(8,128)}, f32[128,512]{1,0:T(8,128)}, /*index=5*/f32[1,4096]{1,0:T(1,128)}) custom-call(s32[32]{0:T(128)} %get-tuple-element.27.other_ref, s32[32]{0:T(128)} %get-tuple-element.26.count_ref, ...), custom_call_target="tpu_custom_call" | custom-call | tf_op jit(solution)/shard_map/attend/pallas_call | solution.py:115
  61.6 62.9 %scatter.1 = (bf16[128,512]{1,0:T(8,128)(2,1)}, bf16[128,512]{1,0:T(8,128)(2,1)}, f32[1,4096]{1,0:T(1,128)}) custom-call(bf16[16,128,512]{2,1,0:T(8,128)(2,1)} %get-tuple-element.18.part_k, bf16[16,128,512]{2,1,0:T(8,128)(2,1)} %get-tuple-element.19.part_v, f32[128,512]{1,0:T(8,128)} %get-tuple-element.20.own_k, f32[128,512]{1,0:T(8,128)} %get-tuple-element.21.own_v, ...), custom_call_target="tpu_custom_call" | custom-call | tf_op jit(solution)/shard_map/scatter/pallas_call | solution.py:358
  124.5 1.6 %copy.14 = bf16[1,128,512]{2,1,0:T(8,128)(2,1)} copy(bf16[1,128,512]{2,1,0:T(8,128)(2,1)} %bitcast.22) | data formatting | bytes 262144
  126.1 1.6 %copy.15 = bf16[1,128,512]{2,1,0:T(8,128)(2,1)} copy(bf16[1,128,512]{2,1,0:T(8,128)(2,1)} %bitcast.21) | data formatting | bytes 262144
  127.7 1.3 %copy.16 = f32[4096]{0:T(1024)} copy(f32[4096]{0:T(1024)} %bitcast.24) | data formatting | bytes 32768
  (1 shorter events, 0.0 us)
Async XLA Ops:
  0.6 0.7 copy-start
